TPU v7x, 32 devices: a whole 2x2x4 slice. The times are simulated.
32 devices in a mesh: texel: 8 (over y, x, core), light: 4 (over z).
Axes of the slice: x: 2, y: 2, z: 4, core: 2. Of those that a mesh axis runs over, the one named last changes fastest.
Arguments:
- tex_feat: bfloat16 [8192, 512], P('texel'), may hold values from -18 to 18
- light_feat: bfloat16 [6144, 512], P('light'), may hold values from -0.25 to 0.25
- sketch: bfloat16 [6144, 256], P('light'), may hold values from -0.078125 to 0.078125
- row_counts: int32 [8], replicated, may hold values from 1 to 1024, 4096 in all
Outputs:
- basis: float32 [8192, 256], P('texel')
- coeffs: float32 [256, 6144], P('texel', 'light')
Inputs may be any that keep to these rules, and one draw needn't show every extreme that they name: row_counts sums to 8 * 512; some entry equals 1024.
All inputs are finite; a program needn't handle non-finite values.
Results may differ from a plain program's by a relative error of at most 0.0034.
Values sent between devices are 32-bit elements; how exact they have to be, the bound alone decides.
A program may use at most 64 MiB of HBM per device.

v0:
```python
import jax
import jax.numpy as jnp
from jax import lax
from jax.sharding import PartitionSpec as P


def on_device(tex_feat, light_feat, sketch, row_counts):
    capacity = tex_feat.shape[0]
    own_count = row_counts[lax.axis_index("texel")]
    valid_total = jnp.sum(row_counts).astype(jnp.float32)
    logits = lax.dot_general(
        tex_feat, light_feat, (((1,), (1,)), ((), ())), preferred_element_type=jnp.float32
    )
    tile_block = jnp.sin(logits).astype(jnp.bfloat16)
    row_valid = (lax.iota(jnp.int32, capacity) < own_count).astype(jnp.float32)
    partial_value = (
        jnp.dot(tile_block, sketch, preferred_element_type=jnp.float32) * row_valid[:, None]
    )
    sketched = lax.psum(partial_value, "light")
    gram_local = jnp.dot(sketched.T, sketched, precision=lax.Precision.HIGHEST)
    gram_matrix = lax.psum(gram_local, "texel") / valid_total
    factor = jnp.linalg.cholesky(gram_matrix)
    basis = jax.scipy.linalg.solve_triangular(factor, sketched.T, lower=True).T
    basis_half = basis.astype(jnp.bfloat16)
    coeffs = lax.psum_scatter(
        lax.dot_general(
            basis_half, tile_block, (((0,), (0,)), ((), ())), preferred_element_type=jnp.float32
        ),
        "texel",
        scatter_dimension=0,
        tiled=True,
    ) / jnp.sqrt(valid_total)
    return (basis, coeffs)


def solution(mesh):
    placed = (P("texel", None), P("light", None), P("light", None), P())
    return jax.shard_map(
        on_device,
        mesh=mesh,
        in_specs=placed,
        out_specs=(P("texel", None), P("texel", "light")),
        check_vma=False,
    )
```

profile of v0, /device:TPU:8, one launch (start us, length us, event | category | flops | bytes accessed | tf_op | source)
XLA Modules:
  0.0 260.4 jit_solution(2642677506085759507)
XLA Ops:
  7.2 1.3 dynamic_slice.3
  8.6 0.6 fusion.10
  9.3 23.0 %sine_convert_fusion = bf16[1024,1536]{1,0:T(8,128)(2,1)S(1)} fusion(bf16[1024,512]{1,0:T(8,128)(2,1)} %param.4, bf16[1536,512]{1,0:T(8,128)(2,1)S(1)} %copy-done), kind=kOutput, calls=%fused_computation.2 | convolution fusion | flops 1612185600 | bytes 5767168 | tf_op jit(solution)/shard_map/dot_general | solution.py:11
  32.2 1.7 copy-done.2
  33.9 1.9 convolution_multiply_fusion
  35.9 53.0 %all-reduce.4.cloned.1.call-done = f32[1024,256]{1,0:T(8,128)} async-done(((f32[1024,256]{1,0:T(8,128)}), f32[1024,256]{1,0:T(8,128)}) %all-reduce.4.cloned.1.call-update) | async-done | bytes 1048592 | tf_op jit(solution)/shard_map/psum | solution.py:19
  88.9 4.1 %fusion.12 = f32[256,256]{0,1:T(8,128)} fusion(f32[1024,256]{1,0:T(8,128)} %all-reduce.4.cloned.1.call-done), kind=kOutput, calls=%fused_computation.37 | convolution fusion | flops 805306368 | bytes 1310720 | tf_op jit(solution)/shard_map/dot_general | solution.py:20
  93.1 0.2 reduce-scatter.2.cloned.1.call-start
  93.3 0.6 reduce_sum.9
  94.6 52.0 %all-reduce.6.cloned.1.call-done = f32[256,256]{0,1:T(8,128)} async-done(((f32[256,256]{0,1:T(8,128)}), f32[256,256]{0,1:T(8,128)}) %all-reduce.6.cloned.1.call-update) | async-done | bytes 262160 | tf_op jit(solution)/shard_map/psum | solution.py:21
  146.6 1.0 broadcast_divide_fusion
  147.7 1.0 fusion.4
  148.7 11.7 %cholesky.50 = f32[128,128]{1,0:T(8,128)S(1)} custom-call(f32[128,128]{1,0:T(8,128)S(1)} %cholesky.118), custom_call_target="Cholesky" | custom-call | tf_op jit(solution)/shard_map/jit(cholesky)/cholesky | solution.py:22
  160.4 9.8 %custom-call.15 = f32[1,128,128]{1,2,0:T(8,128)S(1)} custom-call(f32[1,128,128]{2,1,0:T(8,128)S(1)} %get-tuple-element.25), custom_call_target="InvertDiagBlocksLowerTriangular" | custom-call | tf_op jit(solution)/shard_map/jit(cholesky)/cholesky | solution.py:22
  170.5 0.3 convolution_subtract_fusion.1
  170.8 11.7 %cholesky.105 = f32[128,128]{1,0:T(8,128)S(1)} custom-call(f32[128,128]{1,0:T(8,128)S(1)} %convolution_subtract_fusion.1), custom_call_target="Cholesky" | custom-call | tf_op jit(solution)/shard_map/jit(cholesky)/cholesky | solution.py:22
  182.5 0.7 compare_reduce_fusion
  184.5 4.1 %while.1 = (s32[]{:T(128)}, f32[256,256]{1,0:T(8,128)S(1)}, s32[2,2]{1,0:T(2,128)S(1)}, f32[2,128,128]{2,1,0:T(8,128)S(1)}, s32[]{:T(128)}) while((s32[]{:T(128)}, f32[256,256]{1,0:T(8,128)S(1)}, s32[2,2]{1,0:T(2,128)S(1)}, f32[2,128,128]{2,1,0:T(8,128)S(1)}, s32[]{:T(128)}) %tuple.28), condition=%wide.while_cond, body=%wide.while_body.sunk | while | flops 2 | bytes 131189 | solution.py:23
  184.7 0.6 fusion.25
  185.3 1.4 bitcast_dynamic-update-slice_fusion.2
  186.7 0.6 fusion.25
  187.3 1.4 bitcast_dynamic-update-slice_fusion.2
  188.7 0.6 copy-done.5
  189.3 20.5 %custom-call.16 = f32[2,128,128]{1,2,0:T(8,128)S(1)} custom-call(f32[2,128,128]{2,1,0:T(8,128)} %copy-done.5), custom_call_target="InvertDiagBlocksLowerTriangular" | custom-call | tf_op jit(solution)/shard_map/jit(_solve_triangular)/triangular_solve | solution.py:23
  209.8 0.6 fusion
  210.5 1.0 convolution_subtract_fusion
  211.5 0.6 fusion.6
  212.1 2.2 fusion.2
  214.4 1.1 maximum_bitcast_fusion
  215.4 2.5 copy.8
  218.0 34.2 %reduce-scatter.2.cloned.1.call-done = f32[32,1536]{1,0:T(8,128)} async-done(((f32[256,1536]{1,0:T(8,128)}), f32[32,1536]{1,0:T(8,128)}) %reduce-scatter.2.cloned.1.call-update) | async-done | bytes 196624 | tf_op jit(solution)/shard_map/reduce_scatter | solution.py:25
  252.2 1.6 broadcast_divide_fusion.1
  (29 shorter events, 0.7 us)
Async XLA Ops:
  7.2 2.1 copy-start
  7.2 81.7 %all-reduce.4.cloned.1.call-start = ((), (), s32[]{:S(2)}) async-start(), calls=%async_computation.1 | async-start | bytes 2097152 | tf_op jit(solution)/shard_map/psum | solution.py:19
  9.2 24.7 %copy-start.4 = (bf16[1536,256]{1,0:T(8,128)(2,1)S(1)}, bf16[1536,256]{1,0:T(8,128)(2,1)}, u32[]{:S(2)}) copy-start(bf16[1536,256]{1,0:T(8,128)(2,1)} %param.6) | copy-start | bytes 2359300
  32.2 1.7 copy-start.2
  35.9 57.5 %copy-start.6 = (s32[8]{0:T(128)S(1)}, s32[8]{0:T(128)}, u32[]{:S(2)}) copy-start(s32[8]{0:T(128)} %param.7) | copy-start | bytes 100
  35.9 110.7 %all-reduce.6.cloned.1.call-start = ((), (), s32[]{:S(2)}) async-start(), calls=%async_computation.2 | async-start | bytes 524288 | tf_op jit(solution)/shard_map/psum | solution.py:21
  88.9 120.9 %copy-start.1 = (f32[1024,256]{1,0:T(8,128)S(1)}, f32[1024,256]{1,0:T(8,128)}, u32[]{:S(2)}) copy-start(f32[1024,256]{1,0:T(8,128)} %all-reduce.4.cloned.1.call-done) | copy-start | bytes 3145732
  93.1 159.1 %reduce-scatter.2.cloned.1.call-start = ((), (), s32[]{:S(2)}) async-start(), calls=%async_computation.3 | async-start | bytes 1769472 | tf_op jit(solution)/shard_map/reduce_scatter | solution.py:25
  188.6 0.7 copy-start.5
  209.8 2.3 copy-start.3
Sparse Core Ops, SparseCore 0:
  36.0 52.8 all-reduce.3
  93.2 53.2 all-reduce.5
  214.4 37.7 reduce-scatter.1
where the time goes:
time: 262 us; the launch traced here: 260 us
  waiting for transfers between devices  139 us (53%)
  other arithmetic  60.4 us (23%)
  matrix products  34 us (13%)
  between operations  15.8 us (6%)
  local copies, waits for them, and re-layouts  10.3 us (4%)
    psum x1, waiting for transfers between devices, on_device(): sketched = lax.psum(partial_value, 'light')  53 us
    psum x1, waiting for transfers between devices, on_device(): gram_matrix = lax.psum(gram_local, 'texel') / valid_total  52 us
    reduce_scatter x1, waiting for transfers between devices, on_device(): lax.psum_scatter(lax.dot_general(basis_half, tile_block, (((0,), (0,)), (...  34.2 us
    another operation x6, other arithmetic, on_device(): factor = jnp.linalg.cholesky(gram_matrix)  34 us
    dot_general x1, matrix products, on_device(): lax.dot_general(tex_feat, light_feat, (((1,), (1,)), ((), ())), preferred...  23 us
    another operation x3, other arithmetic, on_device(): basis = jax.scipy.linalg.solve_triangular(factor, sketched.T, lower=True).T  20.5 us
  transfers between devices with their start and end apart: 3, of which 3 were waited for; matrix products, arithmetic and copies ran while one was open for 2% of the time, Pallas kernels for 0%

commit v1 on v0

--- a/solution.py
+++ b/solution.py
@@ -1,7 +1,102 @@
+import functools
+
 import jax
 import jax.numpy as jnp
 from jax import lax
+from jax.experimental import pallas as pl
+from jax.experimental.pallas import tpu as pltpu
 from jax.sharding import PartitionSpec as P
+
+HIGHEST = lax.Precision.HIGHEST
+BLOCK = 64
+INV_TWO_PI = 0.15915494309189535
+TWO_PI_HIGH = 6.28125
+TWO_PI_LOW = 0.001935307179586232
+SINE = (
+    0.9999999944783076,
+    -0.16666664569596037,
+    0.008333310280569169,
+    -0.00019840151040396647,
+    2.752937413742719e-06,
+    -2.4676261406891767e-08,
+    1.344908473337278e-10,
+)
+
+
+def bounded_sine(x):
+    turns = jnp.round(x * INV_TWO_PI)
+    r = (x - turns * TWO_PI_HIGH) - turns * TWO_PI_LOW
+    s = r * r
+    value = jnp.full_like(s, SINE[-1])
+    for coefficient in SINE[-2::-1]:
+        value = value * s + coefficient
+    return value * r
+
+
+def eliminate(block):
+    rows = [block[8 * t : 8 * t + 8, :] for t in range(8)]
+    below = lax.broadcasted_iota(jnp.int32, (8, 128), 0)
+    for p in range(8):
+        columns = {
+            (t, k): jnp.broadcast_to(rows[t][:, 8 * p + k : 8 * p + k + 1], (8, 128))
+            for t in range(p, 8)
+            for k in range(8)
+        }
+        for k in range(8):
+            inverse = 1.0 / jnp.broadcast_to(columns[p, k][k : k + 1, :], (8, 128))
+            pivot_row = jnp.broadcast_to(rows[p][k : k + 1, :], (8, 128))
+            entries = [
+                jnp.broadcast_to(columns[p, later][k : k + 1, :], (8, 128))
+                for later in range(k + 1, 8)
+            ]
+            for t in range(p, 8):
+                factor = columns[t, k] * inverse
+                if t == p:
+                    factor = jnp.where(below > k, factor, 0.0)
+                rows[t] = rows[t] - factor * pivot_row
+                for later in range(k + 1, 8):
+                    columns[t, later] = columns[t, later] - factor * entries[later - k - 1]
+    return jnp.concatenate(rows, axis=0)
+
+
+def factor_inverse(gram_ref, inverse_ref, work_ref):
+    size = gram_ref.shape[0]
+    work_ref[...] = gram_ref[...]
+    row = lax.broadcasted_iota(jnp.int32, (size, size), 0)
+    column = lax.broadcasted_iota(jnp.int32, (size, size), 1)
+    inverse_ref[...] = jnp.where(row == column, 1.0, 0.0).astype(jnp.float32)
+    lane = lax.broadcasted_iota(jnp.int32, (BLOCK, 128), 1)
+    line = lax.broadcasted_iota(jnp.int32, (BLOCK, 128), 0)
+    for start in range(0, size, BLOCK):
+        own = slice(start, start + BLOCK)
+        tile_start = start // 128 * 128
+        tile = work_ref[own, tile_start : tile_start + 128]
+        if start % 128:
+            tile = pltpu.roll(tile, 64, 1)
+        unit = jnp.where(lane - BLOCK == line, 1.0, 0.0)
+        done = eliminate(jnp.where(lane < BLOCK, tile, unit))
+        pivots = jnp.sum(jnp.where(lane == line, done, 0.0), axis=1, keepdims=True)
+        scaled = pltpu.roll(done * lax.rsqrt(pivots), 64, 1)[:, :BLOCK]
+        left = jnp.dot(scaled, work_ref[own, :], precision=HIGHEST, preferred_element_type=jnp.float32)
+        right = jnp.dot(scaled, inverse_ref[own, :], precision=HIGHEST, preferred_element_type=jnp.float32)
+        inverse_ref[own, :] = right
+        rest = size - start - BLOCK
+        if rest:
+            lower = slice(start + BLOCK, size)
+            flipped = left.T[start + BLOCK :, :]
+            work_ref[lower, :] -= jnp.dot(flipped, left, precision=HIGHEST, preferred_element_type=jnp.float32)
+            inverse_ref[lower, :] -= jnp.dot(flipped, right, precision=HIGHEST, preferred_element_type=jnp.float32)
+
+
+def inverse_of_factor(gram):
+    size = gram.shape[0]
+    return pl.pallas_call(
+        factor_inverse,
+        out_shape=jax.ShapeDtypeStruct((size, size), jnp.float32),
+        in_specs=[pl.BlockSpec(memory_space=pltpu.VMEM)],
+        out_specs=pl.BlockSpec(memory_space=pltpu.VMEM),
+        scratch_shapes=[pltpu.VMEM((size, size), jnp.float32)],
+    )(gram)
 
 
 def on_device(tex_feat, light_feat, sketch, row_counts):
@@ -11,16 +106,16 @@
     logits = lax.dot_general(
         tex_feat, light_feat, (((1,), (1,)), ((), ())), preferred_element_type=jnp.float32
     )
-    tile_block = jnp.sin(logits).astype(jnp.bfloat16)
+    tile_block = bounded_sine(logits).astype(jnp.bfloat16)
     row_valid = (lax.iota(jnp.int32, capacity) < own_count).astype(jnp.float32)
     partial_value = (
         jnp.dot(tile_block, sketch, preferred_element_type=jnp.float32) * row_valid[:, None]
     )
     sketched = lax.psum(partial_value, "light")
-    gram_local = jnp.dot(sketched.T, sketched, precision=lax.Precision.HIGHEST)
+    gram_local = jnp.dot(sketched.T, sketched, precision=HIGHEST)
     gram_matrix = lax.psum(gram_local, "texel") / valid_total
-    factor = jnp.linalg.cholesky(gram_matrix)
-    basis = jax.scipy.linalg.solve_triangular(factor, sketched.T, lower=True).T
+    inverse = inverse_of_factor(gram_matrix)
+    basis = lax.dot_general(sketched, inverse, (((1,), (1,)), ((), ())), precision=HIGHEST)
     basis_half = basis.astype(jnp.bfloat16)
     coeffs = lax.psum_scatter(
         lax.dot_general(

time: 262 us -> 199 us (0.76)
  other arithmetic: 60.4 us -> 4.58 us
  matrix products: 34 us -> 19.1 us
  Pallas kernels: 0 us -> 11.4 us
  local copies, waits for them, and re-layouts: 10.3 us -> 3.98 us
  waiting for transfers between devices: 139 us -> 143 us
    another operation x9 -> x0, other arithmetic: 54.5 us -> none  [the longest x6 34 us: on_device(): factor = jnp.linalg.cholesky(gram_matrix)]
    dot_general x1, matrix products: 23 us -> 6.97 us  [on_device(): lax.dot_general(tex_feat, light_feat, (((1,), (1,)), ((), ())), preferred...]
    pallas_call x0 -> x1, Pallas kernels: none -> 11.4 us  [inverse_of_factor(): pl.pallas_call(factor_inverse, out_shape=jax.ShapeDtypeStruct((size, size...]
    another operation x9 -> x0, local copies, waits for them, and re-layouts: 3.99 us -> none
    reduce_scatter x1, waiting for transfers between devices: 34.2 us -> 37.8 us  [on_device(): lax.psum_scatter(lax.dot_general(basis_half, tile_block, (((0,), (0,)), (...]
    another operation x5 -> x0, matrix products: 2.75 us -> none  [the longest x3 2.28 us: on_device(): basis = jax.scipy.linalg.solve_triangular(factor, sketched.T, lower=True).T]
    dot_general x1 -> x2, matrix products: 4.15 us -> 6.13 us  [the longest x1 4.15 us: on_device(): gram_local = jnp.dot(sketched.T, sketched, precision=HIGHEST)]
  transfers between devices with their start and end apart: 3 -> 3, of which waited for: 3 -> 3; matrix products, arithmetic and copies ran while one was open for 2% -> 0% of each run, Pallas kernels for 0% -> 0%
where the time goes in v1:
time: 199 us; the launch traced here: 197 us
  waiting for transfers between devices  143 us (72%)
  matrix products  19.1 us (10%)
  between operations  14.5 us (7%)
  Pallas kernels  11.4 us (6%)
  other arithmetic  4.58 us (2%)
  local copies, waits for them, and re-layouts  3.98 us (2%)
    psum x1, waiting for transfers between devices, on_device(): sketched = lax.psum(partial_value, 'light')  53 us
    psum x1, waiting for transfers between devices, on_device(): gram_matrix = lax.psum(gram_local, 'texel') / valid_total  51.9 us
    reduce_scatter x1, waiting for transfers between devices, on_device(): lax.psum_scatter(lax.dot_general(basis_half, tile_block, (((0,), (0,)), (...  37.8 us
    pallas_call x1, Pallas kernels, inverse_of_factor(): pl.pallas_call(factor_inverse, out_shape=jax.ShapeDtypeStruct((size, size...  11.4 us
    dot_general x1, matrix products, on_device(): lax.dot_general(tex_feat, light_feat, (((1,), (1,)), ((), ())), preferred...  6.97 us
    dot_general x1, matrix products, on_device(): gram_local = jnp.dot(sketched.T, sketched, precision=HIGHEST)  4.15 us
    dot_general x1, matrix products, on_device(): lax.dot_general(basis_half, tile_block, (((0,), (0,)), ((), ())), preferr...  4.08 us
  transfers between devices with their start and end apart: 3, of which 3 were waited for; matrix products, arithmetic and copies ran while one was open for 0% of the time, Pallas kernels for 0%

profile of v1, /device:TPU:8, one launch (start us, length us, event | category | flops | bytes accessed | tf_op | source)
XLA Modules:
  0.0 196.7 jit_solution(16240319977960494201)
XLA Ops:
  7.2 0.0 copy-start
  7.2 0.0 all-reduce.3.cloned.1.call-start
  7.2 1.3 dynamic_slice.3
  8.6 0.6 fusion.6
  9.2 0.0 copy-done
  9.2 0.0 copy-start.4
  9.3 7.0 %multiply_convert_fusion = bf16[1024,1536]{1,0:T(8,128)(2,1)S(1)} fusion(bf16[1024,512]{1,0:T(8,128)(2,1)} %param.4, bf16[1536,512]{1,0:T(8,128)(2,1)S(1)} %copy-done), kind=kOutput, calls=%fused_computation | convolution fusion | flops 1643642880 | bytes 5767168 | tf_op jit(solution)/shard_map/dot_general | solution.py:106
  16.2 0.0 copy-start.3
  16.2 1.6 copy-done.3
  17.9 0.0 copy-done.4
  17.9 1.9 convolution_multiply_fusion
  19.8 0.0 copy-start.5
  19.8 0.0 all-reduce.3.cloned.1.call-update
  19.9 0.0 all-reduce.5.cloned.1.call-start
  19.9 53.0 %all-reduce.3.cloned.1.call-done = f32[1024,256]{1,0:T(8,128)} async-done(((f32[1024,256]{1,0:T(8,128)}), f32[1024,256]{1,0:T(8,128)}) %all-reduce.3.cloned.1.call-update) | async-done | bytes 1048592 | tf_op jit(solution)/shard_map/psum | solution.py:114
  72.9 0.0 copy-start.1
  72.9 4.2 %fusion.7 = f32[256,256]{1,0:T(8,128)} fusion(f32[1024,256]{1,0:T(8,128)} %all-reduce.3.cloned.1.call-done), kind=kOutput, calls=%fused_computation.16 | convolution fusion | flops 805306368 | bytes 1310720 | tf_op jit(solution)/shard_map/dot_general | solution.py:115
  77.1 0.0 all-reduce.5.cloned.1.call-update
  77.1 0.2 reduce-scatter.2.cloned.1.call-start
  77.3 0.0 copy-done.5
  77.3 0.6 reduce_sum.9
  78.6 51.9 %all-reduce.5.cloned.1.call-done = f32[256,256]{1,0:T(8,128)} async-done(((f32[256,256]{1,0:T(8,128)}), f32[256,256]{1,0:T(8,128)}) %all-reduce.5.cloned.1.call-update) | async-done | bytes 262160 | tf_op jit(solution)/shard_map/psum | solution.py:116
  130.6 1.7 broadcast_divide_fusion.gram_ref
  132.2 11.4 %shard_map.59 = f32[256,256]{1,0:T(8,128)} custom-call(f32[256,256]{1,0:T(8,128)} %broadcast_divide_fusion.gram_ref), custom_call_target="tpu_custom_call" | custom-call | tf_op jit(solution)/shard_map/pallas_call | solution.py:93
  143.6 0.0 copy-done.1
  143.6 2.0 %fusion.8 = f32[1024,256]{1,0:T(8,128)S(1)} fusion(f32[1024,256]{1,0:T(8,128)S(1)} %copy-done.1, f32[256,256]{1,0:T(8,128)} %shard_map.59), kind=kOutput, calls=%fused_computation.17 | convolution fusion | flops 805306368 | bytes 2359296 | tf_op jit(solution)/shard_map/dot_general | solution.py:118
  145.6 0.0 copy-start.2
  145.6 1.0 copy-done.2
  146.6 4.1 %fusion.4 = f32[256,1536]{1,0:T(8,128)} fusion(bf16[1024,1536]{1,0:T(8,128)(2,1)} %copy-done.3, f32[1024,256]{1,0:T(8,128)S(1)} %fusion.8), kind=kOutput, calls=%fused_computation.10 | convolution fusion | flops 805568512 | bytes 5767168 | tf_op jit(solution)/shard_map/dot_general | solution.py:121
  150.7 0.0 reduce-scatter.2.cloned.1.call-update
  150.8 37.8 %reduce-scatter.2.cloned.1.call-done = f32[32,1536]{1,0:T(8,128)} async-done(((f32[256,1536]{1,0:T(8,128)}), f32[32,1536]{1,0:T(8,128)}) %reduce-scatter.2.cloned.1.call-update) | async-done | bytes 196624 | tf_op jit(solution)/shard_map/reduce_scatter | solution.py:120
  188.6 1.6 broadcast_divide_fusion.1
Async XLA Ops:
  7.2 2.1 %copy-start = (bf16[1536,512]{1,0:T(8,128)(2,1)S(1)}, bf16[1536,512]{1,0:T(8,128)(2,1)}, u32[]{:S(2)}) copy-start(bf16[1536,512]{1,0:T(8,128)(2,1)} %param.5) | copy-start | bytes 4718596
  7.2 65.7 %all-reduce.3.cloned.1.call-start = ((), (), s32[]{:S(2)}) async-start(), calls=%async_computation.1 | async-start | bytes 2097152 | tf_op jit(solution)/shard_map/psum | solution.py:114
  9.2 8.6 %copy-start.4 = (bf16[1536,256]{1,0:T(8,128)(2,1)S(1)}, bf16[1536,256]{1,0:T(8,128)(2,1)}, u32[]{:S(2)}) copy-start(bf16[1536,256]{1,0:T(8,128)(2,1)} %param.6) | copy-start | bytes 2359300
  16.2 1.6 copy-start.3
  19.8 57.5 %copy-start.5 = (s32[8]{0:T(128)S(1)}, s32[8]{0:T(128)}, u32[]{:S(2)}) copy-start(s32[8]{0:T(128)} %param.7) | copy-start | bytes 100
  19.9 110.7 %all-reduce.5.cloned.1.call-start = ((), (), s32[]{:S(2)}) async-start(), calls=%async_computation.2 | async-start | bytes 524288 | tf_op jit(solution)/shard_map/psum | solution.py:116
  72.9 70.7 %copy-start.1 = (f32[1024,256]{1,0:T(8,128)S(1)}, f32[1024,256]{1,0:T(8,128)}, u32[]{:S(2)}) copy-start(f32[1024,256]{1,0:T(8,128)} %all-reduce.3.cloned.1.call-done) | copy-start | bytes 3145732
  77.1 111.5 %reduce-scatter.2.cloned.1.call-start = ((), (), s32[]{:S(2)}) async-start(), calls=%async_computation.3 | async-start | bytes 1769472 | tf_op jit(solution)/shard_map/reduce_scatter | solution.py:120
  145.6 1.0 copy-start.2
Sparse Core Ops, SparseCore 0:
  20.0 52.8 all-reduce.2
  77.2 53.2 all-reduce.4
  150.8 37.6 reduce-scatter.1

commit v2 on v1

--- a/solution.py
+++ b/solution.py
@@ -99,7 +99,221 @@
     )(gram)
 
 
-def on_device(tex_feat, light_feat, sketch, row_counts):
+MESH_ID = pl.DeviceIdType.MESH
+
+
+def greet(peers):
+    barrier = pltpu.get_barrier_semaphore()
+    for peer in peers:
+        pl.semaphore_signal(barrier, inc=1, device_id=peer, device_id_type=MESH_ID)
+    pl.semaphore_wait(barrier, len(peers))
+
+
+def sketch_and_gram(
+    n_texel, n_light, partial_ref, whole_ref, gram_ref,
+    landed, whole, pieces, plane, column, gram,
+    part_send, part_recv, plane_send, plane_recv, column_send, column_recv,
+    full_send, full_recv, row_send, row_recv,
+):
+    texel, light = lax.axis_index("texel"), lax.axis_index("light")
+    depth = partial_ref.shape[0] // n_light
+    size = partial_ref.shape[1]
+    piece = size // n_texel
+    lights = [lax.rem(light + d, n_light) for d in range(n_light)]
+    texels = [lax.rem(texel + d, n_texel) for d in range(n_texel)]
+    greet([(texel, lights[d]) for d in range(1, n_light)] + [(texels[d], light) for d in range(1, n_texel)])
+
+    def send(source, target, send_sem, recv_sem, device):
+        copy = pltpu.make_async_remote_copy(
+            src_ref=source, dst_ref=target, send_sem=send_sem, recv_sem=recv_sem,
+            device_id=device, device_id_type=MESH_ID,
+        )
+        copy.start()
+        return copy
+
+    def rows_of(index, height):
+        return pl.ds(pl.multiple_of(index * height, height), height)
+
+    copies = [
+        send(
+            partial_ref.at[rows_of(lights[d], depth)], landed.at[d],
+            part_send.at[d], part_recv.at[d], (texel, lights[d]),
+        )
+        for d in range(1, n_light)
+    ]
+    own = partial_ref[rows_of(light, depth), :]
+    for d, copy in enumerate(copies, 1):
+        copy.wait()
+        own = own + landed[d]
+    whole[rows_of(light, depth), :] = own
+
+    local = lax.dot_general(
+        own, own, (((0,), (0,)), ((), ())), precision=HIGHEST, preferred_element_type=jnp.float32
+    )
+    for index in range(n_texel):
+        pieces[index] = local[index * piece : (index + 1) * piece, :]
+    copies = [
+        send(pieces.at[texels[d]], plane.at[d], plane_send.at[d], plane_recv.at[d], (texels[d], light))
+        for d in range(1, n_texel)
+    ]
+    total = pieces[texel]
+    for d, copy in enumerate(copies, 1):
+        copy.wait()
+        total = total + plane[d]
+    column[light] = total
+    copies = [
+        send(column.at[light], column.at[light], column_send.at[d], column_recv.at[d], (texel, lights[d]))
+        for d in range(1, n_light)
+    ]
+    for copy in copies:
+        copy.wait()
+    gathers = [
+        send(
+            whole.at[rows_of(light, depth)], whole.at[rows_of(light, depth)],
+            full_send.at[d], full_recv.at[d], (texel, lights[d]),
+        )
+        for d in range(1, n_light)
+    ]
+    total = column[0]
+    for index in range(1, n_light):
+        total = total + column[index]
+    gram[rows_of(texel, piece), :] = total
+    copies = [
+        send(
+            gram.at[rows_of(texel, piece)], gram.at[rows_of(texel, piece)],
+            row_send.at[d], row_recv.at[d], (texels[d], light),
+        )
+        for d in range(1, n_texel)
+    ]
+    for copy in copies:
+        copy.wait()
+    gram_ref[...] = gram[...]
+    for copy in gathers:
+        copy.wait()
+    whole_ref[...] = whole[...]
+
+
+def reduced(partial, n_texel, n_light):
+    capacity, size = partial.shape
+    depth, piece = capacity // n_light, size // n_texel
+    vmem = pl.BlockSpec(memory_space=pltpu.VMEM)
+    f32 = jnp.float32
+    sems = pltpu.SemaphoreType.DMA
+    return pl.pallas_call(
+        functools.partial(sketch_and_gram, n_texel, n_light),
+        out_shape=(
+            jax.ShapeDtypeStruct((capacity, size), f32),
+            jax.ShapeDtypeStruct((size, size), f32),
+        ),
+        in_specs=[vmem],
+        out_specs=(vmem, vmem),
+        scratch_shapes=[
+            pltpu.VMEM((n_light, depth, size), f32),
+            pltpu.VMEM((capacity, size), f32),
+            pltpu.VMEM((n_texel, piece, size), f32),
+            pltpu.VMEM((n_texel, piece, size), f32),
+            pltpu.VMEM((n_light, piece, size), f32),
+            pltpu.VMEM((size, size), f32),
+            sems((n_light,)), sems((n_light,)),
+            sems((n_texel,)), sems((n_texel,)),
+            sems((n_light,)), sems((n_light,)),
+            sems((n_light,)), sems((n_light,)),
+            sems((n_texel,)), sems((n_texel,)),
+        ],
+        compiler_params=pltpu.CompilerParams(collective_id=1, has_side_effects=True),
+    )(partial)
+
+
+def halving_order(bits, last_first):
+    rest = list(range(1, bits))
+    return [0] + (rest[::-1] if last_first else rest)
+
+
+def scatter_sum(n_texel, partial_ref, out_ref, held, landed, send_sem, recv_sem):
+    texel, light = lax.axis_index("texel"), lax.axis_index("light")
+    bits = n_texel.bit_length() - 1
+    bit = [lax.rem(texel // (1 << b), 2) for b in range(bits)]
+    partner = [texel + (1 - 2 * bit[b]) * (1 << b) for b in range(bits)]
+    greet([(partner[b], light) for b in range(bits)])
+    piece = partial_ref.shape[0] // n_texel
+    width = partial_ref.shape[1] // 2
+
+    def start_of(mask):
+        block = 0
+        for b in range(bits):
+            flipped = 1 - bit[b] if mask >> b & 1 else bit[b]
+            block = block + flipped * (1 << b)
+        return pl.multiple_of(block * piece, piece)
+
+    orders = [halving_order(bits, False), halving_order(bits, True)]
+    flights = [{}, {}]
+    for step in range(bits):
+        for half, order in enumerate(orders):
+            b = order[step]
+            left = [m for m in range(n_texel) if all(not m >> done & 1 for done in order[:step])]
+            later = order[step + 1 :]
+            going = [m for m in left if m >> b & 1]
+            going.sort(key=lambda m: [-(m >> c & 1) for c in later])
+            columns = pl.ds(half * width, width)
+            for m in going:
+                kept = m - (1 << b)
+                if step == 0:
+                    source = partial_ref.at[pl.ds(start_of(m), piece), columns]
+                else:
+                    arrived = flights[half].pop((step - 1, m))
+                    arrived.wait()
+                    below = (
+                        partial_ref[pl.ds(start_of(m), piece), columns] if step == 1 else held[half, m]
+                    )
+                    held[half, m] = below + landed[half, step - 1, m]
+                    source = held.at[half, m]
+                copy = pltpu.make_async_remote_copy(
+                    src_ref=source,
+                    dst_ref=landed.at[half, step, kept],
+                    send_sem=send_sem.at[half, step, kept],
+                    recv_sem=recv_sem.at[half, step, kept],
+                    device_id=(partner[b], light),
+                    device_id_type=MESH_ID,
+                )
+                copy.start()
+                flights[half][step, kept] = copy
+        if step:
+            for half, order in enumerate(orders):
+                for key in [k for k in flights[half] if k[0] == step - 1]:
+                    m = key[1]
+                    flights[half].pop(key).wait()
+                    columns = pl.ds(half * width, width)
+                    below = (
+                        partial_ref[pl.ds(start_of(m), piece), columns] if step == 1 else held[half, m]
+                    )
+                    held[half, m] = below + landed[half, step - 1, m]
+    for half in range(2):
+        columns = pl.ds(half * width, width)
+        flights[half].pop((bits - 1, 0)).wait()
+        below = partial_ref[pl.ds(start_of(0), piece), columns] if bits == 1 else held[half, 0]
+        out_ref[:, half * width : (half + 1) * width] = below + landed[half, bits - 1, 0]
+
+
+def scattered(partial, n_texel):
+    size, lights = partial.shape
+    piece, width, bits = size // n_texel, lights // 2, n_texel.bit_length() - 1
+    vmem = pl.BlockSpec(memory_space=pltpu.VMEM)
+    return pl.pallas_call(
+        functools.partial(scatter_sum, n_texel),
+        out_shape=jax.ShapeDtypeStruct((piece, lights), jnp.float32),
+        in_specs=[vmem],
+        out_specs=vmem,
+        scratch_shapes=[
+            pltpu.VMEM((2, n_texel, piece, width), jnp.float32),
+            pltpu.VMEM((2, bits, n_texel, piece, width), jnp.float32),
+            pltpu.SemaphoreType.DMA((2, bits, n_texel)),
+            pltpu.SemaphoreType.DMA((2, bits, n_texel)),
+        ],
+        compiler_params=pltpu.CompilerParams(collective_id=2, has_side_effects=True),
+    )(partial)
+
+
+def on_device(n_texel, n_light, tex_feat, light_feat, sketch, row_counts):
     capacity = tex_feat.shape[0]
     own_count = row_counts[lax.axis_index("texel")]
     valid_total = jnp.sum(row_counts).astype(jnp.float32)
@@ -111,27 +325,22 @@
     partial_value = (
         jnp.dot(tile_block, sketch, preferred_element_type=jnp.float32) * row_valid[:, None]
     )
-    sketched = lax.psum(partial_value, "light")
-    gram_local = jnp.dot(sketched.T, sketched, precision=HIGHEST)
-    gram_matrix = lax.psum(gram_local, "texel") / valid_total
+    sketched, gram_sum = reduced(partial_value, n_texel, n_light)
+    gram_matrix = gram_sum / valid_total
     inverse = inverse_of_factor(gram_matrix)
     basis = lax.dot_general(sketched, inverse, (((1,), (1,)), ((), ())), precision=HIGHEST)
     basis_half = basis.astype(jnp.bfloat16)
-    coeffs = lax.psum_scatter(
-        lax.dot_general(
-            basis_half, tile_block, (((0,), (0,)), ((), ())), preferred_element_type=jnp.float32
-        ),
-        "texel",
-        scatter_dimension=0,
-        tiled=True,
-    ) / jnp.sqrt(valid_total)
+    partial_coeffs = lax.dot_general(
+        basis_half, tile_block, (((0,), (0,)), ((), ())), preferred_element_type=jnp.float32
+    )
+    coeffs = scattered(partial_coeffs, n_texel) / jnp.sqrt(valid_total)
     return (basis, coeffs)
 
 
 def solution(mesh):
     placed = (P("texel", None), P("light", None), P("light", None), P())
     return jax.shard_map(
-        on_device,
+        functools.partial(on_device, mesh.shape["texel"], mesh.shape["light"]),
         mesh=mesh,
         in_specs=placed,
         out_specs=(P("texel", None), P("texel", "light")),

time: 199 us -> 114 us (0.57); the launches traced: 197 us -> 114 us
  waiting for transfers between devices: 143 us -> 0 us
  Pallas kernels: 11.4 us -> 88.5 us
  between operations: 14.5 us -> 1.42 us
  matrix products: 19.1 us -> 15.6 us
    psum x2 -> x0, waiting for transfers between devices: 105 us -> none  [the longest x1 53 us: on_device(): sketched = lax.psum(partial_value, 'light')]
    pallas_call x0 -> x2, Pallas kernels: none -> 77.1 us  [the longest x1 62.1 us: reduced(): pl.pallas_call(functools.partial(sketch_and_gram, n_texel, n_light), out_...]
    reduce_scatter x1 -> x0, waiting for transfers between devices: 37.8 us -> none  [on_device(): lax.psum_scatter(lax.dot_general(basis_half, tile_block, (((0,), (0,)), (...]
    dot_general x1 -> x0, matrix products: 4.15 us -> none  [on_device(): gram_local = jnp.dot(sketched.T, sketched, precision=HIGHEST)]
  transfers between devices with their start and end apart: 3 -> 0, of which waited for: 3 -> 0; matrix products, arithmetic and copies ran while one was open for 0% -> 0% of each run, Pallas kernels for 0% -> 0%
where the time goes in v2:
time: 114 us
  Pallas kernels  88.5 us (78%)
  matrix products  15.6 us (14%)
  other arithmetic  5.36 us (5%)
  local copies, waits for them, and re-layouts  2.91 us (3%)
  between operations  1.42 us (1%)
    pallas_call x1, Pallas kernels, reduced(): pl.pallas_call(functools.partial(sketch_and_gram, n_texel, n_light), out_...  62.1 us
    pallas_call x1, Pallas kernels, scattered(): pl.pallas_call(functools.partial(scatter_sum, n_texel), out_shape=jax.Sha...  15 us
    pallas_call x1, Pallas kernels, inverse_of_factor(): pl.pallas_call(factor_inverse, out_shape=jax.ShapeDtypeStruct((size, size...  11.4 us
    dot_general x1, matrix products, on_device(): lax.dot_general(tex_feat, light_feat, (((1,), (1,)), ((), ())), preferred...  6.98 us
    dot_general x1, matrix products, on_device(): lax.dot_general(basis_half, tile_block, (((0,), (0,)), ((), ())), preferr...  4.42 us
    dot_general x1, matrix products, on_device(): lax.dot_general(sketched, inverse, (((1,), (1,)), ((), ())), precision=HI...  2.28 us

profile of v2, /device:TPU:8, one launch (start us, length us, event | category | flops | bytes accessed | tf_op | source)
XLA Modules:
  0.0 113.8 jit_solution(12824572137255445327)
XLA Ops:
  0.6 0.0 copy-start
  0.6 1.4 %reduce_sum.9 = s32[]{:T(128)} reduce(s32[8]{0:T(128)} %param.7, s32[]{:T(128)} %constant.28.clone.1), dimensions={0}, to_apply=%region_0.0 | reduce | flops 7 | bytes 40 | tf_op jit(solution)/shard_map/reduce_sum | solution.py:319
  2.8 1.2 %dynamic_slice.3 = s32[1]{0:T(128)} dynamic-slice(s32[8]{0:T(128)} %param.7, s32[]{:T(128)S(6)} %select_n.3), dynamic_slice_sizes={1} | dynamic-slice | bytes 12 | tf_op jit(solution)/shard_map/dynamic_slice | solution.py:318
  4.0 0.6 fusion.6
  4.7 0.0 copy-done
  4.7 0.0 copy-start.3
  4.7 7.0 %multiply_convert_fusion = bf16[1024,1536]{1,0:T(8,128)(2,1)S(1)} fusion(bf16[1024,512]{1,0:T(8,128)(2,1)} %param.4, bf16[1536,512]{1,0:T(8,128)(2,1)S(1)} %copy-done), kind=kOutput, calls=%fused_computation | convolution fusion | flops 1643642880 | bytes 5767168 | tf_op jit(solution)/shard_map/dot_general | solution.py:320
  11.7 0.0 copy-start.2
  11.7 1.6 %copy-done.2 = bf16[1024,1536]{1,0:T(8,128)(2,1)} copy-done((bf16[1024,1536]{1,0:T(8,128)(2,1)}, bf16[1024,1536]{1,0:T(8,128)(2,1)S(1)}, u32[]{:S(2)}) %copy-start.2) | copy-done | bytes 3145752
  13.3 0.0 copy-done.3
  13.3 1.9 %convolution_multiply_fusion.partial_ref = f32[1024,256]{1,0:T(8,128)} fusion(bf16[1024,1536]{1,0:T(8,128)(2,1)S(1)} %multiply_convert_fusion, bf16[1536,256]{1,0:T(8,128)(2,1)S(1)} %copy-done.3, f32[1024]{0:T(1024)S(1)} %fusion.6), kind=kOutput, calls=%fused_computation.9 | convolution fusion | flops 805568512 | bytes 4984832 | tf_op jit(solution)/shard_map/dot_general | solution.py:326
  15.3 62.1 %shard_map.59 = (f32[1024,256]{1,0:T(8,128)}, f32[256,256]{1,0:T(8,128)}) custom-call(f32[1024,256]{1,0:T(8,128)} %convolution_multiply_fusion.partial_ref), custom_call_target="tpu_custom_call" | custom-call | tf_op jit(solution)/shard_map/pallas_call | solution.py:202
  77.4 1.7 %broadcast_divide_fusion.gram_ref = f32[256,256]{1,0:T(8,128)} fusion(f32[256,256]{1,0:T(8,128)} %get-tuple-element.5, f32[]{:T(128)S(6)} %convert_element_type.18), kind=kLoop, calls=%fused_computation.12 | loop fusion | flops 65536 | bytes 524292 | tf_op jit(solution)/shard_map/div | solution.py:329
  79.1 11.4 %shard_map.60 = f32[256,256]{1,0:T(8,128)} custom-call(f32[256,256]{1,0:T(8,128)} %broadcast_divide_fusion.gram_ref), custom_call_target="tpu_custom_call" | custom-call | tf_op jit(solution)/shard_map/pallas_call | solution.py:93
  90.5 2.3 %fusion.7 = f32[1024,256]{1,0:T(8,128)S(1)} fusion(f32[1024,256]{1,0:T(8,128)} %get-tuple-element.4, f32[256,256]{1,0:T(8,128)} %shard_map.60), kind=kOutput, calls=%fused_computation.16 | convolution fusion | flops 805306368 | bytes 2359296 | tf_op jit(solution)/shard_map/dot_general | solution.py:331
  92.8 0.0 copy-start.1
  92.8 4.4 %fusion.4.partial_ref = f32[256,1536]{1,0:T(8,128)} fusion(bf16[1024,1536]{1,0:T(8,128)(2,1)} %copy-done.2, f32[1024,256]{1,0:T(8,128)S(1)} %fusion.7), kind=kOutput, calls=%fused_computation.10 | convolution fusion | flops 805568512 | bytes 5767168 | tf_op jit(solution)/shard_map/dot_general | solution.py:333
  97.2 15.0 %shard_map.61 = f32[32,1536]{1,0:T(8,128)} custom-call(f32[256,1536]{1,0:T(8,128)} %fusion.4.partial_ref), custom_call_target="tpu_custom_call" | custom-call | tf_op jit(solution)/shard_map/pallas_call | solution.py:301
  112.2 0.0 copy-done.1
  112.2 1.6 %broadcast_divide_fusion.1 = f32[32,1536]{1,0:T(8,128)} fusion(f32[32,1536]{1,0:T(8,128)} %shard_map.61, f32[]{:T(128)S(6)} %sqrt.3), kind=kLoop, calls=%fused_computation.13 | loop fusion | flops 49152 | bytes 393220 | tf_op jit(solution)/shard_map/div | solution.py:336
Async XLA Ops:
  0.6 4.0 %copy-start = (bf16[1536,512]{1,0:T(8,128)(2,1)S(1)}, bf16[1536,512]{1,0:T(8,128)(2,1)}, u32[]{:S(2)}) copy-start(bf16[1536,512]{1,0:T(8,128)(2,1)} %param.5) | copy-start | bytes 4718596
  4.7 8.7 %copy-start.3 = (bf16[1536,256]{1,0:T(8,128)(2,1)S(1)}, bf16[1536,256]{1,0:T(8,128)(2,1)}, u32[]{:S(2)}) copy-start(bf16[1536,256]{1,0:T(8,128)(2,1)} %param.6) | copy-start | bytes 2359300
  11.7 1.7 %copy-start.2 = (bf16[1024,1536]{1,0:T(8,128)(2,1)}, bf16[1024,1536]{1,0:T(8,128)(2,1)S(1)}, u32[]{:S(2)}) copy-start(bf16[1024,1536]{1,0:T(8,128)(2,1)S(1)} %multiply_convert_fusion) | copy-start | bytes 9437188
  92.8 19.4 %copy-start.1 = (f32[1024,256]{1,0:T(8,128)}, f32[1024,256]{1,0:T(8,128)S(1)}, u32[]{:S(2)}) copy-start(f32[1024,256]{1,0:T(8,128)S(1)} %fusion.7) | copy-start | bytes 3145732

commit v3 on v2

--- a/solution.py
+++ b/solution.py
@@ -88,17 +88,6 @@
             inverse_ref[lower, :] -= jnp.dot(flipped, right, precision=HIGHEST, preferred_element_type=jnp.float32)
 
 
-def inverse_of_factor(gram):
-    size = gram.shape[0]
-    return pl.pallas_call(
-        factor_inverse,
-        out_shape=jax.ShapeDtypeStruct((size, size), jnp.float32),
-        in_specs=[pl.BlockSpec(memory_space=pltpu.VMEM)],
-        out_specs=pl.BlockSpec(memory_space=pltpu.VMEM),
-        scratch_shapes=[pltpu.VMEM((size, size), jnp.float32)],
-    )(gram)
-
-
 MESH_ID = pl.DeviceIdType.MESH
 
 
@@ -110,8 +99,8 @@
 
 
 def sketch_and_gram(
-    n_texel, n_light, partial_ref, whole_ref, gram_ref,
-    landed, whole, pieces, plane, column, gram,
+    n_texel, n_light, partial_ref, count_ref, whole_ref, inverse_ref,
+    landed, whole, pieces, plane, column, gram, scaled, work,
     part_send, part_recv, plane_send, plane_recv, column_send, column_recv,
     full_send, full_recv, row_send, row_recv,
 ):
@@ -146,7 +135,18 @@
         copy.wait()
         own = own + landed[d]
     whole[rows_of(light, depth), :] = own
-
+    early = depth // 4
+
+    def gather(part, first, height):
+        rows = pl.ds(pl.multiple_of(light * depth + first, 8), height)
+        return [
+            send(
+                whole.at[rows], whole.at[rows], full_send.at[part, d], full_recv.at[part, d], (texel, lights[d])
+            )
+            for d in range(1, n_light)
+        ]
+
+    gathers = gather(0, 0, early)
     local = lax.dot_general(
         own, own, (((0,), (0,)), ((), ())), precision=HIGHEST, preferred_element_type=jnp.float32
     )
@@ -167,13 +167,7 @@
     ]
     for copy in copies:
         copy.wait()
-    gathers = [
-        send(
-            whole.at[rows_of(light, depth)], whole.at[rows_of(light, depth)],
-            full_send.at[d], full_recv.at[d], (texel, lights[d]),
-        )
-        for d in range(1, n_light)
-    ]
+    gathers += gather(1, early, depth - early)
     total = column[0]
     for index in range(1, n_light):
         total = total + column[index]
@@ -187,13 +181,14 @@
     ]
     for copy in copies:
         copy.wait()
-    gram_ref[...] = gram[...]
+    scaled[...] = gram[...] / count_ref[...]
+    factor_inverse(scaled, inverse_ref, work)
     for copy in gathers:
         copy.wait()
     whole_ref[...] = whole[...]
 
 
-def reduced(partial, n_texel, n_light):
+def reduced(partial, count, n_texel, n_light):
     capacity, size = partial.shape
     depth, piece = capacity // n_light, size // n_texel
     vmem = pl.BlockSpec(memory_space=pltpu.VMEM)
@@ -205,7 +200,7 @@
             jax.ShapeDtypeStruct((capacity, size), f32),
             jax.ShapeDtypeStruct((size, size), f32),
         ),
-        in_specs=[vmem],
+        in_specs=[vmem, vmem],
         out_specs=(vmem, vmem),
         scratch_shapes=[
             pltpu.VMEM((n_light, depth, size), f32),
@@ -214,14 +209,16 @@
             pltpu.VMEM((n_texel, piece, size), f32),
             pltpu.VMEM((n_light, piece, size), f32),
             pltpu.VMEM((size, size), f32),
+            pltpu.VMEM((size, size), f32),
+            pltpu.VMEM((size, size), f32),
             sems((n_light,)), sems((n_light,)),
             sems((n_texel,)), sems((n_texel,)),
             sems((n_light,)), sems((n_light,)),
-            sems((n_light,)), sems((n_light,)),
+            sems((2, n_light)), sems((2, n_light)),
             sems((n_texel,)), sems((n_texel,)),
         ],
         compiler_params=pltpu.CompilerParams(collective_id=1, has_side_effects=True),
-    )(partial)
+    )(partial, count)
 
 
 def halving_order(bits, last_first):
@@ -325,9 +322,8 @@
     partial_value = (
         jnp.dot(tile_block, sketch, preferred_element_type=jnp.float32) * row_valid[:, None]
     )
-    sketched, gram_sum = reduced(partial_value, n_texel, n_light)
-    gram_matrix = gram_sum / valid_total
-    inverse = inverse_of_factor(gram_matrix)
+    count = jnp.full((1, partial_value.shape[1]), valid_total)
+    sketched, inverse = reduced(partial_value, count, n_texel, n_light)
     basis = lax.dot_general(sketched, inverse, (((1,), (1,)), ((), ())), precision=HIGHEST)
     basis_half = basis.astype(jnp.bfloat16)
     partial_coeffs = lax.dot_general(

time: 114 us -> 100 us (0.88)
  Pallas kernels: 88.5 us -> 75.4 us
  other arithmetic: 5.36 us -> 3.68 us
    pallas_call x1 -> x0, Pallas kernels: 11.4 us -> none  [inverse_of_factor(): pl.pallas_call(factor_inverse, out_shape=jax.ShapeDtypeStruct((size, size...]
    div x1 -> x0, other arithmetic: 1.68 us -> none  [on_device(): gram_matrix = gram_sum / valid_total]
where the time goes in v3:
time: 100 us; the launch traced here: 99.6 us
  Pallas kernels  75.4 us (75%)
  matrix products  15.6 us (16%)
  other arithmetic  3.68 us (4%)
  local copies, waits for them, and re-layouts  3.47 us (3%)
  between operations  1.42 us (1%)
    pallas_call x1, Pallas kernels, reduced(): pl.pallas_call(functools.partial(sketch_and_gram, n_texel, n_light), out_...  61.2 us
    pallas_call x1, Pallas kernels, scattered(): pl.pallas_call(functools.partial(scatter_sum, n_texel), out_shape=jax.Sha...  14.3 us
    dot_general x1, matrix products, on_device(): lax.dot_general(tex_feat, light_feat, (((1,), (1,)), ((), ())), preferred...  6.98 us
    dot_general x1, matrix products, on_device(): lax.dot_general(basis_half, tile_block, (((0,), (0,)), ((), ())), preferr...  4.42 us
    dot_general x1, matrix products, on_device(): lax.dot_general(sketched, inverse, (((1,), (1,)), ((), ())), precision=HI...  2.29 us

profile of v3, /device:TPU:8, one launch (start us, length us, event | category | flops | bytes accessed | tf_op | source)
XLA Modules:
  0.0 99.6 jit_solution(15705086179110386017)
XLA Ops:
  0.6 0.0 copy-start
  0.6 1.4 %reduce_sum.9 = s32[]{:T(128)} reduce(s32[8]{0:T(128)} %param.7, s32[]{:T(128)} %constant.28.clone.1), dimensions={0}, to_apply=%region_0.0 | reduce | flops 7 | bytes 40 | tf_op jit(solution)/shard_map/reduce_sum | solution.py:316
  2.8 1.2 %dynamic_slice.3 = s32[1]{0:T(128)} dynamic-slice(s32[8]{0:T(128)} %param.7, s32[]{:T(128)S(6)} %select_n.3), dynamic_slice_sizes={1} | dynamic-slice | bytes 12 | tf_op jit(solution)/shard_map/dynamic_slice | solution.py:315
  4.0 0.6 broadcast_in_dim.8.count_ref
  4.6 0.6 fusion.6
  5.2 0.0 copy-done
  5.2 0.0 copy-start.3
  5.2 7.0 %multiply_convert_fusion = bf16[1024,1536]{1,0:T(8,128)(2,1)S(1)} fusion(bf16[1024,512]{1,0:T(8,128)(2,1)} %param.4, bf16[1536,512]{1,0:T(8,128)(2,1)S(1)} %copy-done), kind=kOutput, calls=%fused_computation | convolution fusion | flops 1643642880 | bytes 5767168 | tf_op jit(solution)/shard_map/dot_general | solution.py:317
  12.2 0.0 copy-start.2
  12.2 1.6 %copy-done.2 = bf16[1024,1536]{1,0:T(8,128)(2,1)} copy-done((bf16[1024,1536]{1,0:T(8,128)(2,1)}, bf16[1024,1536]{1,0:T(8,128)(2,1)S(1)}, u32[]{:S(2)}) %copy-start.2) | copy-done | bytes 3145752
  13.9 0.0 copy-done.3
  13.9 1.9 %convolution_multiply_fusion.partial_ref = f32[1024,256]{1,0:T(8,128)} fusion(bf16[1024,1536]{1,0:T(8,128)(2,1)S(1)} %multiply_convert_fusion, bf16[1536,256]{1,0:T(8,128)(2,1)S(1)} %copy-done.3, f32[1024]{0:T(1024)S(1)} %fusion.6), kind=kOutput, calls=%fused_computation.9 | convolution fusion | flops 805568512 | bytes 4984832 | tf_op jit(solution)/shard_map/dot_general | solution.py:323
  15.8 61.2 %shard_map.59 = (f32[1024,256]{1,0:T(8,128)}, f32[256,256]{1,0:T(8,128)}) custom-call(f32[1024,256]{1,0:T(8,128)} %convolution_multiply_fusion.partial_ref, f32[1,256]{1,0:T(1,128)} %broadcast_in_dim.8.count_ref), custom_call_target="tpu_custom_call" | custom-call | tf_op jit(solution)/shard_map/pallas_call | solution.py:197
  77.0 2.3 %fusion.7 = f32[1024,256]{1,0:T(8,128)S(1)} fusion(f32[1024,256]{1,0:T(8,128)} %get-tuple-element.4, f32[256,256]{1,0:T(8,128)} %get-tuple-element.5), kind=kOutput, calls=%fused_computation.15 | convolution fusion | flops 805306368 | bytes 2359296 | tf_op jit(solution)/shard_map/dot_general | solution.py:327
  79.3 0.0 copy-start.1
  79.3 4.4 %fusion.4.partial_ref = f32[256,1536]{1,0:T(8,128)} fusion(bf16[1024,1536]{1,0:T(8,128)(2,1)} %copy-done.2, f32[1024,256]{1,0:T(8,128)S(1)} %fusion.7), kind=kOutput, calls=%fused_computation.10 | convolution fusion | flops 805568512 | bytes 5767168 | tf_op jit(solution)/shard_map/dot_general | solution.py:329
  83.7 14.3 %shard_map.60 = f32[32,1536]{1,0:T(8,128)} custom-call(f32[256,1536]{1,0:T(8,128)} %fusion.4.partial_ref), custom_call_target="tpu_custom_call" | custom-call | tf_op jit(solution)/shard_map/pallas_call | solution.py:298
  98.0 0.0 copy-done.1
  98.0 1.6 %broadcast_divide_fusion = f32[32,1536]{1,0:T(8,128)} fusion(f32[32,1536]{1,0:T(8,128)} %shard_map.60, f32[]{:T(128)S(6)} %sqrt.3), kind=kLoop, calls=%fused_computation.12 | loop fusion | flops 49152 | bytes 393220 | tf_op jit(solution)/shard_map/div | solution.py:332
Async XLA Ops:
  0.6 4.6 %copy-start = (bf16[1536,512]{1,0:T(8,128)(2,1)S(1)}, bf16[1536,512]{1,0:T(8,128)(2,1)}, u32[]{:S(2)}) copy-start(bf16[1536,512]{1,0:T(8,128)(2,1)} %param.5) | copy-start | bytes 4718596
  5.2 8.7 %copy-start.3 = (bf16[1536,256]{1,0:T(8,128)(2,1)S(1)}, bf16[1536,256]{1,0:T(8,128)(2,1)}, u32[]{:S(2)}) copy-start(bf16[1536,256]{1,0:T(8,128)(2,1)} %param.6) | copy-start | bytes 2359300
  12.2 1.7 %copy-start.2 = (bf16[1024,1536]{1,0:T(8,128)(2,1)}, bf16[1024,1536]{1,0:T(8,128)(2,1)S(1)}, u32[]{:S(2)}) copy-start(bf16[1024,1536]{1,0:T(8,128)(2,1)S(1)} %multiply_convert_fusion) | copy-start | bytes 9437188
  79.3 18.7 %copy-start.1 = (f32[1024,256]{1,0:T(8,128)}, f32[1024,256]{1,0:T(8,128)S(1)}, u32[]{:S(2)}) copy-start(f32[1024,256]{1,0:T(8,128)S(1)} %fusion.7) | copy-start | bytes 3145732

commit v4 on v3

--- a/solution.py
+++ b/solution.py
@@ -99,7 +99,8 @@
 
 
 def sketch_and_gram(
-    n_texel, n_light, partial_ref, count_ref, whole_ref, inverse_ref,
+    n_texel, n_light, tex_ref, feat_ref, sketch_ref, used_ref, count_ref, whole_ref, inverse_ref, tile_ref,
+    logits, partial_ref,
     landed, whole, pieces, plane, column, gram, scaled, work,
     part_send, part_recv, plane_send, plane_recv, column_send, column_recv,
     full_send, full_recv, row_send, row_recv,
@@ -123,13 +124,40 @@
     def rows_of(index, height):
         return pl.ds(pl.multiple_of(index * height, height), height)
 
-    copies = [
-        send(
-            partial_ref.at[rows_of(lights[d], depth)], landed.at[d],
-            part_send.at[d], part_recv.at[d], (texel, lights[d]),
+    step = logits.shape[1]
+
+    def fill(index):
+        texels_here = tex_ref[rows_of(index, depth), :]
+
+        def block(c, carry):
+            columns = rows_of(c, step)
+            logits[...] = lax.dot_general(
+                texels_here, feat_ref[columns, :], (((1,), (1,)), ((), ())), preferred_element_type=jnp.float32
+            )
+
+            def strip(i, inner):
+                value = bounded_sine(logits[rows_of(i, 16), :]).astype(jnp.bfloat16)
+                tile_ref[pl.ds(pl.multiple_of(index * depth + i * 16, 16), 16), columns] = value
+                return inner
+
+            return lax.fori_loop(0, depth // 16, strip, carry, unroll=2)
+
+        lax.fori_loop(0, feat_ref.shape[0] // step, block, 0)
+        rows = rows_of(index, depth)
+        partial_ref[rows, :] = (
+            jnp.dot(tile_ref[rows, :], sketch_ref[...], preferred_element_type=jnp.float32) * used_ref[rows, :]
         )
-        for d in range(1, n_light)
-    ]
+
+    copies = []
+    for d in range(1, n_light):
+        fill(lights[d])
+        copies.append(
+            send(
+                partial_ref.at[rows_of(lights[d], depth)], landed.at[d],
+                part_send.at[d], part_recv.at[d], (texel, lights[d]),
+            )
+        )
+    fill(light)
     own = partial_ref[rows_of(light, depth), :]
     for d, copy in enumerate(copies, 1):
         copy.wait()
@@ -188,8 +216,10 @@
     whole_ref[...] = whole[...]
 
 
-def reduced(partial, count, n_texel, n_light):
-    capacity, size = partial.shape
+def reduced(tex_feat, light_feat, sketch, used, count, n_texel, n_light):
+    capacity, size = tex_feat.shape[0], sketch.shape[1]
+    lights = light_feat.shape[0]
+    step = next(w for w in (512, 256, 128) if lights % w == 0)
     depth, piece = capacity // n_light, size // n_texel
     vmem = pl.BlockSpec(memory_space=pltpu.VMEM)
     f32 = jnp.float32
@@ -199,10 +229,13 @@
         out_shape=(
             jax.ShapeDtypeStruct((capacity, size), f32),
             jax.ShapeDtypeStruct((size, size), f32),
+            jax.ShapeDtypeStruct((capacity, lights), jnp.bfloat16),
         ),
-        in_specs=[vmem, vmem],
-        out_specs=(vmem, vmem),
+        in_specs=[vmem] * 5,
+        out_specs=(vmem, vmem, vmem),
         scratch_shapes=[
+            pltpu.VMEM((depth, step), f32),
+            pltpu.VMEM((capacity, size), f32),
             pltpu.VMEM((n_light, depth, size), f32),
             pltpu.VMEM((capacity, size), f32),
             pltpu.VMEM((n_texel, piece, size), f32),
@@ -218,7 +251,7 @@
             sems((n_texel,)), sems((n_texel,)),
         ],
         compiler_params=pltpu.CompilerParams(collective_id=1, has_side_effects=True),
-    )(partial, count)
+    )(tex_feat, light_feat, sketch, used, count)
 
 
 def halving_order(bits, last_first):
@@ -314,16 +347,11 @@
     capacity = tex_feat.shape[0]
     own_count = row_counts[lax.axis_index("texel")]
     valid_total = jnp.sum(row_counts).astype(jnp.float32)
-    logits = lax.dot_general(
-        tex_feat, light_feat, (((1,), (1,)), ((), ())), preferred_element_type=jnp.float32
+    row_valid = (lax.iota(jnp.int32, capacity) < own_count).astype(jnp.float32)
+    count = jnp.full((1, sketch.shape[1]), valid_total)
+    sketched, inverse, tile_block = reduced(
+        tex_feat, light_feat, sketch, row_valid[:, None], count, n_texel, n_light
     )
-    tile_block = bounded_sine(logits).astype(jnp.bfloat16)
-    row_valid = (lax.iota(jnp.int32, capacity) < own_count).astype(jnp.float32)
-    partial_value = (
-        jnp.dot(tile_block, sketch, preferred_element_type=jnp.float32) * row_valid[:, None]
-    )
-    count = jnp.full((1, partial_value.shape[1]), valid_total)
-    sketched, inverse = reduced(partial_value, count, n_texel, n_light)
     basis = lax.dot_general(sketched, inverse, (((1,), (1,)), ((), ())), precision=HIGHEST)
     basis_half = basis.astype(jnp.bfloat16)
     partial_coeffs = lax.dot_general(

time: 100 us -> 93.1 us (0.931)
  matrix products: 15.6 us -> 6.69 us
  Pallas kernels: 75.4 us -> 78.4 us
  local copies, waits for them, and re-layouts: 3.47 us -> 1.89 us
    dot_general x2 -> x0, matrix products: 8.92 us -> none  [the longest x1 6.98 us: on_device(): lax.dot_general(tex_feat, light_feat, (((1,), (1,)), ((), ())), preferred...]
    pallas_call x1, Pallas kernels: 61.2 us -> 64.3 us  [reduced(): pl.pallas_call(functools.partial(sketch_and_gram, n_texel, n_light), out_...]
    unnamed x8 -> x2, local copies, waits for them, and re-layouts: 1.67 us -> 0.01 us
where the time goes in v4:
time: 93.1 us; the launch traced here: 92.8 us
  Pallas kernels  78.4 us (84%)
  matrix products  6.69 us (7%)
  other arithmetic  4.45 us (5%)
  local copies, waits for them, and re-layouts  1.89 us (2%)
  between operations  1.37 us (1%)
    pallas_call x1, Pallas kernels, reduced(): pl.pallas_call(functools.partial(sketch_and_gram, n_texel, n_light), out_...  64.3 us
    pallas_call x1, Pallas kernels, scattered(): pl.pallas_call(functools.partial(scatter_sum, n_texel), out_shape=jax.Sha...  14 us
    dot_general x1, matrix products, on_device(): lax.dot_general(basis_half, tile_block, (((0,), (0,)), ((), ())), preferr...  4.4 us
    dot_general x1, matrix products, on_device(): lax.dot_general(sketched, inverse, (((1,), (1,)), ((), ())), precision=HI...  2.29 us

profile of v4, /device:TPU:8, one launch (start us, length us, event | category | flops | bytes accessed | tf_op | source)
XLA Modules:
  0.0 92.8 jit_solution(9944441451946981493)
XLA Ops:
  0.6 1.3 %reduce_sum.9 = s32[]{:T(128)} reduce(s32[8]{0:T(128)} %param.7, s32[]{:T(128)} %constant.8.clone.1), dimensions={0}, to_apply=%region_0.0 | reduce | flops 7 | bytes 40 | tf_op jit(solution)/shard_map/reduce_sum | solution.py:349
  2.6 1.3 %dynamic_slice.3 = s32[1]{0:T(128)} dynamic-slice(s32[8]{0:T(128)} %param.7, s32[]{:T(128)S(6)} %select_n.3), dynamic_slice_sizes={1} | dynamic-slice | bytes 12 | tf_op jit(solution)/shard_map/dynamic_slice | solution.py:348
  3.9 0.6 broadcast_in_dim.4.count_ref
  4.5 1.5 %fusion.2.used_ref = f32[1024,1]{1,0:T(8,128)} fusion(s32[]{:T(128)} %bitcast), kind=kLoop, calls=%fused_computation.3 | loop fusion | flops 2048 | bytes 4100 | tf_op jit(solution)/shard_map/convert_element_type | solution.py:350
  6.0 64.3 %shard_map.59 = (f32[1024,256]{1,0:T(8,128)}, f32[256,256]{1,0:T(8,128)}, bf16[1024,1536]{1,0:T(8,128)(2,1)}) custom-call(bf16[1024,512]{1,0:T(8,128)(2,1)} %tex_ref.1, bf16[1536,512]{1,0:T(8,128)(2,1)} %feat_ref.1, bf16[1536,256]{1,0:T(8,128)(2,1)} %sketch_ref.1, f32[1024,1]{1,0:T(8,128)} %fusion.2.used_ref, f32[1,256]{1,0:T(1,128)} %broadcast_in_dim.4.count_ref), custom_call_target="tpu_custom_call" | custom-call | tf_op jit(solution)/shard_map/pallas_call | solution.py:227
  70.4 2.3 %fusion.3 = f32[1024,256]{1,0:T(8,128)S(1)} fusion(f32[1024,256]{1,0:T(8,128)} %get-tuple-element.5, f32[256,256]{1,0:T(8,128)} %get-tuple-element.6), kind=kOutput, calls=%fused_computation.5 | convolution fusion | flops 805306368 | bytes 2359296 | tf_op jit(solution)/shard_map/dot_general | solution.py:355
  72.7 0.0 copy-start
  72.7 4.4 %fusion.partial_ref = f32[256,1536]{1,0:T(8,128)} fusion(bf16[1024,1536]{1,0:T(8,128)(2,1)} %get-tuple-element.7, f32[1024,256]{1,0:T(8,128)S(1)} %fusion.3), kind=kOutput, calls=%fused_computation | convolution fusion | flops 805568512 | bytes 5767168 | tf_op jit(solution)/shard_map/dot_general | solution.py:357
  77.1 14.0 %shard_map.60 = f32[32,1536]{1,0:T(8,128)} custom-call(f32[256,1536]{1,0:T(8,128)} %fusion.partial_ref), custom_call_target="tpu_custom_call" | custom-call | tf_op jit(solution)/shard_map/pallas_call | solution.py:331
  91.2 0.0 copy-done
  91.2 1.6 %broadcast_divide_fusion = f32[32,1536]{1,0:T(8,128)} fusion(f32[32,1536]{1,0:T(8,128)} %shard_map.60, f32[]{:T(128)S(6)} %sqrt.3), kind=kLoop, calls=%fused_computation.4 | loop fusion | flops 49152 | bytes 393220 | tf_op jit(solution)/shard_map/div | solution.py:360
Async XLA Ops:
  72.7 18.5 %copy-start = (f32[1024,256]{1,0:T(8,128)}, f32[1024,256]{1,0:T(8,128)S(1)}, u32[]{:S(2)}) copy-start(f32[1024,256]{1,0:T(8,128)S(1)} %fusion.3) | copy-start | bytes 3145732
